TPU v7x, 32 devices: a whole 2x2x4 slice. The times are simulated.
32 devices in a mesh: clip: 2 (over x), tm: 16 (over z, y, core).
Axes of the slice: x: 2, y: 2, z: 4, core: 2. Of those that a mesh axis runs over, the one named last changes fastest.
Arguments:
- frames: bfloat16 [64, 1024, 256], P('tm', 'clip'), parts along dimension 1, may hold values from -6 to 6
- gain_one: float32 [256], replicated, may hold values from 0.25 to 1.75
- conv_one: bfloat16 [3, 3, 3, 256, 256], replicated, may hold values from -0.078125 to 0.078125
- gain_two: float32 [256], replicated, may hold values from 0.25 to 1.75
- conv_two: bfloat16 [3, 3, 3, 256, 256], replicated, may hold values from -0.078125 to 0.078125
- out_weight: bfloat16 [256, 256], replicated, may hold values from -0.375 to 0.375
Outputs:
- latent: bfloat16 [64, 1024, 256], P(None, ('clip', 'tm')), parts along dimension 1
There are 2 independent parts, one for each index of `clip`. A program takes and returns all parts, laid end to end along the dimension named above; an argument that names none is the same for every part. Nothing has to cross between parts.
All inputs are finite; a program needn't handle non-finite values.
Results may differ from a plain program's by a relative error of at most 0.0065.
Values may be sent and summed in bfloat16 or wider, within the bound.
A program may use at most 192 MiB of HBM per device.

v0:
```python
import functools

import jax
import jax.numpy as jnp
from jax import lax
from jax.experimental import pallas as pl
from jax.experimental.pallas import tpu as pltpu
from jax.sharding import PartitionSpec as P

ROWS = 4
COLS = 128
MESH = pl.DeviceIdType.MESH


def norm_act(x, gain):
    values = x.astype(jnp.float32)
    scale = lax.rsqrt(jnp.mean(values * values, axis=-1, keepdims=True) + 1e-06)
    scaled = values * scale * gain
    return scaled * (0.5 * jnp.tanh(0.5 * scaled) + 0.5)


def store_shifted(acts, frame, row, act):
    channels = act.shape[-1]
    place = lax.broadcasted_iota(jnp.int32, act.shape, 0)
    before = jnp.where(place == 0, 0.0, pltpu.roll(act, 1, 0))
    after = jnp.where(place == COLS - 1, 0.0, pltpu.roll(act, COLS - 1, 0))
    acts[frame, row, :, :channels] = before.astype(jnp.bfloat16)
    acts[frame, row, :, channels : 2 * channels] = act.astype(jnp.bfloat16)
    acts[frame, row, :, 2 * channels :] = after.astype(jnp.bfloat16)


def conv_row(acts, kernel, frame, source, tap, rows):
    total = None
    for tap_t in range(3):
        for at in range(rows):
            window = acts[pl.ds(frame + tap_t, 2), source + at]
            part = jnp.dot(
                window.reshape(2 * COLS, window.shape[-1]),
                kernel[tap_t * 3 + tap + at],
                preferred_element_type=jnp.float32,
            )
            total = part if total is None else total + part
    return total.reshape(2, COLS, total.shape[-1])


def both_rows(acts, kernel, frame, half):
    border = conv_row(acts, kernel, frame, 2 * half, 1 - half, 2)
    inner = conv_row(acts, kernel, frame, half, 0, 3)
    return (((ROWS - 1) * half, border), (1 + half, inner))


def fused(
    n,
    frames_ref,
    gain_one,
    conv_one,
    gain_two,
    conv_two,
    out_weight,
    out_ref,
    frames,
    halo_one,
    halo_two,
    edge_two,
    kernel_one,
    kernel_two,
    project,
    acts_one,
    acts_two,
    first,
    result,
    load_sems,
    halo_send,
    halo_recv,
    edge_send,
    edge_recv,
    out_send,
    out_recv,
    own_sem,
):
    me = lax.axis_index("tm")
    count = frames.shape[0]
    channels = frames.shape[-1]
    owned = result.shape[2]
    per_row = COLS // owned
    earlier = me - 1
    later = me + 1

    loads = [pltpu.make_async_copy(frames_ref, frames, load_sems.at[0])]
    for source, target in ((conv_one, kernel_one), (conv_two, kernel_two)):
        for tap in range(9):
            sem = load_sems.at[len(loads)]
            loads.append(pltpu.make_async_copy(source.at[tap], target.at[tap], sem))
    loads.append(pltpu.make_async_copy(out_weight, project, load_sems.at[19]))
    for load in loads[:10]:
        load.start()

    barrier = pltpu.get_barrier_semaphore()

    @pl.loop(1, n)
    def _(step):
        pl.semaphore_signal(
            barrier, inc=1, device_id={"tm": lax.rem(me + step, n)}, device_id_type=MESH
        )

    loads[0].wait()

    @pl.loop(0, count * ROWS)
    def _(index):
        frame = index // ROWS
        row = index % ROWS
        act = norm_act(frames[frame, row], gain_one[...])
        store_shifted(acts_one, frame + 2, row, act)

    pl.semaphore_wait(barrier, n - 1)

    halo_copy = pltpu.make_async_remote_copy(
        src_ref=frames_ref.at[pl.ds(count - 2, 2)],
        dst_ref=halo_one,
        send_sem=halo_send,
        recv_sem=halo_recv,
        device_id={"tm": lax.rem(later, n)},
        device_id_type=MESH,
    )

    def edge_copy(row):
        return pltpu.make_async_remote_copy(
            src_ref=edge_two.at[row],
            dst_ref=halo_two.at[row],
            send_sem=edge_send.at[row],
            recv_sem=edge_recv.at[row],
            device_id={"tm": lax.rem(later, n)},
            device_id_type=MESH,
        )

    @pl.when(later < n)
    def _():
        halo_copy.start()

    for load in loads[1:10]:
        load.wait()
    for load in loads[10:]:
        load.start()

    halves = ROWS // 2
    pairs = count // 2
    steps = pairs * halves
    far = 1 - (2 * me) // n

    def finish(frame, row, conv):
        value = (first[pl.ds(frame, 2), row].astype(jnp.float32) + conv).astype(jnp.bfloat16)
        latent = jnp.dot(
            value.reshape(2 * COLS, channels),
            project[...],
            preferred_element_type=jnp.float32,
        ).astype(jnp.bfloat16)
        for at in range(2):
            for index in range(per_row):
                begin = at * COLS + index * owned
                result[row * per_row + index, frame + at] = latent[begin : begin + owned]

    @pl.loop(0, halves)
    def _(stage):

        @pl.loop(stage * (steps - 1), steps - 1 + stage)
        def _(step):
            frame = count - 2 - 2 * (step // halves)
            near = (far + step) % halves
            head = step == steps - halves

            @pl.when(head & (me > 0))
            def _():
                halo_copy.wait_recv()

                @pl.loop(0, 2 * ROWS)
                def _(index):
                    at = index // ROWS
                    row = index % ROWS
                    store_shifted(acts_one, at, row, norm_act(halo_one[at, row], gain_one[...]))

            @pl.when(head & (me == 0))
            def _():
                @pl.loop(0, 2 * ROWS)
                def _(index):
                    blank = jnp.zeros((COLS, acts_one.shape[-1]), jnp.bfloat16)
                    acts_one[index // ROWS, index % ROWS] = blank
                    acts_two[index // ROWS, index % ROWS] = blank

            for row, conv in both_rows(acts_one, kernel_one, frame, near):
                for at in range(2):
                    value = (frames[frame + at, row].astype(jnp.float32) + conv[at]).astype(
                        jnp.bfloat16
                    )
                    first[frame + at, row] = value
                    store_shifted(acts_two, frame + at + 2, row, norm_act(value, gain_two[...]))

            @pl.when((step < halves) & (later < n))
            def _():
                for row in ((ROWS - 1) * near, 1 + near):
                    for at in range(2):
                        edge_two[row, at] = acts_two[count + at, row, :, channels : 2 * channels]
                    edge_copy(row).start()

        @pl.when(stage == 0)
        def _():
            for load in loads[10:]:
                load.wait()

        @pl.loop(stage * pairs, (3 * stage + 1) * pairs)
        def _(step):
            unit = step // pairs
            frame = count - 2 - 2 * (step % pairs)
            half = (far + unit // 2) % halves
            inner = unit % 2

            @pl.when((step == pairs - 1) & (me > 0))
            def _():
                @pl.loop(0, ROWS)
                def _(row):
                    edge_copy(row).wait_recv()
                    for at in range(2):
                        store_shifted(acts_two, at, row, halo_two[row, at].astype(jnp.float32))

            @pl.when(inner == 0)
            def _():
                conv = conv_row(acts_two, kernel_two, frame, 2 * half, 1 - half, 2)
                finish(frame, (ROWS - 1) * half, conv)

            @pl.when(inner == 1)
            def _():
                finish(frame, 1 + half, conv_row(acts_two, kernel_two, frame, half, 0, 3))

            row = 2 * half + (half + inner) % 2

            @pl.loop(0, per_row)
            def _(index):
                owner = row * per_row + index

                @pl.when(owner != me)
                def _():
                    pltpu.make_async_remote_copy(
                        src_ref=result.at[owner, pl.ds(frame, 2)],
                        dst_ref=out_ref.at[pl.ds(me * count + frame, 2)],
                        send_sem=out_send,
                        recv_sem=out_recv,
                        device_id={"tm": owner},
                        device_id_type=MESH,
                    ).start()

    own = pltpu.make_async_copy(result.at[me], out_ref.at[pl.ds(me * count, count)], own_sem)
    own.start()

    @pl.when(later < n)
    def _():
        halo_copy.wait_send()
        for row in range(ROWS):
            edge_copy(row).wait_send()

    others = out_ref.at[pl.ds(0, (n - 1) * count)]
    sent = result.at[pl.ds(0, n - 1)]
    pltpu.make_async_copy(sent, sent, out_send).wait()
    pltpu.make_async_copy(others, others, out_recv).wait()
    own.wait()


def body(n, frames, gain_one, conv_one, gain_two, conv_two, out_weight):
    count, cells, channels = frames.shape
    owned = cells // n
    grid = (count, ROWS, COLS, channels)
    taps = (9, 3 * channels, channels)
    half = jnp.bfloat16
    hbm = pl.BlockSpec(memory_space=pl.ANY)
    vmem = pl.BlockSpec(memory_space=pltpu.VMEM)
    return pl.pallas_call(
        functools.partial(fused, n),
        out_shape=jax.ShapeDtypeStruct((n * count, owned, channels), half),
        in_specs=[hbm, vmem, hbm, vmem, hbm, hbm],
        out_specs=hbm,
        scratch_shapes=[
            pltpu.VMEM(grid, half),
            pltpu.VMEM((2, ROWS, COLS, channels), half),
            pltpu.VMEM((ROWS, 2, COLS, channels), half),
            pltpu.VMEM((ROWS, 2, COLS, channels), half),
            pltpu.VMEM(taps, half),
            pltpu.VMEM(taps, half),
            pltpu.VMEM((channels, channels), half),
            pltpu.VMEM((count + 2, ROWS, COLS, 3 * channels), half),
            pltpu.VMEM((count + 2, ROWS, COLS, 3 * channels), half),
            pltpu.VMEM(grid, half),
            pltpu.VMEM((n, count, owned, channels), half),
            pltpu.SemaphoreType.DMA((20,)),
            pltpu.SemaphoreType.DMA,
            pltpu.SemaphoreType.DMA,
            pltpu.SemaphoreType.DMA((ROWS,)),
            pltpu.SemaphoreType.DMA((ROWS,)),
            pltpu.SemaphoreType.DMA,
            pltpu.SemaphoreType.DMA,
            pltpu.SemaphoreType.DMA,
        ],
        compiler_params=pltpu.CompilerParams(collective_id=0, has_side_effects=True),
    )(
        frames.reshape(grid),
        gain_one.reshape(1, channels),
        conv_one.reshape(taps),
        gain_two.reshape(1, channels),
        conv_two.reshape(taps),
        out_weight,
    )


def solution(mesh):
    placed = (P("tm", "clip", None), P(), P(), P(), P(), P())
    return jax.shard_map(
        functools.partial(body, mesh.shape["tm"]),
        mesh=mesh,
        in_specs=placed,
        out_specs=P(None, ("clip", "tm"), None),
        check_vma=False,
    )
```

profile of v0, /device:TPU:17, one launch (start us, length us, event | category | flops | bytes accessed | tf_op | source)
XLA Modules:
  0.0 41.9 jit_solution(9766874837494537816)
XLA Ops:
  0.0 39.6 %shard_map.64 = bf16[64,32,256]{2,1,0:T(8,128)(2,1)} custom-call(bf16[4,4,128,256]{3,2,1,0:T(8,128)(2,1)} %bitcast.7, f32[1,256]{1,0:T(1,128)} %bitcast.8, bf16[9,768,256]{2,1,0:T(8,128)(2,1)} %bitcast.5, f32[1,256]{1,0:T(1,128)} %bitcast.9, bf16[9,768,256]{2,1,0:T(8,128)(2,1)} %bitcast.6, bf16[256,256]{1,0:T(8,128)(2,1)} %out_weight.1), custom_call_target="tpu_custom_call" | custom-call | tf_op jit(solution)/shard_map/pallas_call | solution.py:274
  39.6 2.3 %copy.8 = bf16[64,32,256]{2,1,0:T(8,128)(2,1)} copy(bf16[64,32,256]{2,1,0:T(8,128)(2,1)} %shard_map.64) | data formatting | bytes 2097152
where the time goes:
time: 42.3 us; the launch traced here: 41.9 us
  Pallas kernels  39.6 us (94%)
  local copies, waits for them, and re-layouts  2.26 us (5%)
    pallas_call x1, Pallas kernels, body(): pl.pallas_call(functools.partial(fused, n), out_shape=jax.ShapeDtypeStruc...  39.6 us
    unnamed x1, local copies, waits for them, and re-layouts  2.26 us

commit v1 on v0

--- a/solution.py
+++ b/solution.py
@@ -273,7 +273,7 @@
     vmem = pl.BlockSpec(memory_space=pltpu.VMEM)
     return pl.pallas_call(
         functools.partial(fused, n),
-        out_shape=jax.ShapeDtypeStruct((n * count, owned, channels), half),
+        out_shape=pltpu.VMEM((n * count, owned, channels), half),
         in_specs=[hbm, vmem, hbm, vmem, hbm, hbm],
         out_specs=hbm,
         scratch_shapes=[

time: 42.3 us -> 40.9 us (0.967)
  local copies, waits for them, and re-layouts: 2.26 us -> 0.97 us
    unnamed x1, local copies, waits for them, and re-layouts: 2.26 us -> 0.97 us
where the time goes in v1:
time: 40.9 us; the launch traced here: 40.5 us
  Pallas kernels  39.5 us (97%)
  local copies, waits for them, and re-layouts  0.97 us (2%)
    pallas_call x1, Pallas kernels, body(): pl.pallas_call(functools.partial(fused, n), out_shape=pltpu.VMEM((n * cou...  39.5 us
    unnamed x1, local copies, waits for them, and re-layouts  0.97 us

profile of v1, /device:TPU:17, one launch (start us, length us, event | category | flops | bytes accessed | tf_op | source)
XLA Modules:
  0.0 40.5 jit_solution(8735338965270336520)
XLA Ops:
  0.0 39.5 %shard_map.64 = bf16[64,32,256]{2,1,0:T(8,128)(2,1)S(1)} custom-call(bf16[4,4,128,256]{3,2,1,0:T(8,128)(2,1)} %bitcast.7, f32[1,256]{1,0:T(1,128)} %bitcast.8, bf16[9,768,256]{2,1,0:T(8,128)(2,1)} %bitcast.5, f32[1,256]{1,0:T(1,128)} %bitcast.9, bf16[9,768,256]{2,1,0:T(8,128)(2,1)} %bitcast.6, bf16[256,256]{1,0:T(8,128)(2,1)} %out_weight.1), custom_call_target="tpu_custom_call" | custom-call | tf_op jit(solution)/shard_map/pallas_call | solution.py:274
  39.5 1.0 %copy.8 = bf16[64,32,256]{2,1,0:T(8,128)(2,1)} copy(bf16[64,32,256]{2,1,0:T(8,128)(2,1)S(1)} %shard_map.64) | data formatting | bytes 2097152

commit v2 on v1

v2 whole, which is shorter than its diff:
```python
import functools

import jax
import jax.numpy as jnp
from jax import lax
from jax.experimental import pallas as pl
from jax.experimental.pallas import tpu as pltpu
from jax.sharding import PartitionSpec as P

ROWS = 4
COLS = 128
MESH = pl.DeviceIdType.MESH
DIRECT = ((1, 0), (1, 1), (1, 2), (0, 0), (0, 1), (0, 2), (1, 3), (0, 3))
RELAYED = ((1, 3), (0, 3))
RELAYED_EDGES = (3, 2)


def norm_act(x, half_gain):
    values = x.astype(jnp.float32)
    scale = lax.rsqrt(jnp.mean(values * values, axis=-1, keepdims=True) + 1e-06)
    half = values * scale * half_gain
    return half + half * jnp.tanh(half)


def store_shifted(acts, frame, pos, act):
    channels = act.shape[-1]
    place = lax.broadcasted_iota(jnp.int32, act.shape, 0)
    before = jnp.where(place == 0, 0.0, pltpu.roll(act, 1, 0))
    after = jnp.where(place == COLS - 1, 0.0, pltpu.roll(act, COLS - 1, 0))
    acts[frame, pos, :, :channels] = before.astype(jnp.bfloat16)
    acts[frame, pos, :, channels : 2 * channels] = act.astype(jnp.bfloat16)
    acts[frame, pos, :, 2 * channels :] = after.astype(jnp.bfloat16)


def fused(
    n,
    frames_ref,
    gain_one,
    conv_one,
    gain_two,
    conv_two,
    out_weight,
    out_ref,
    frames,
    halo,
    edges,
    relay,
    kernel_one,
    kernel_two,
    project,
    acts_one,
    acts_two,
    first,
    result,
    frame_sems,
    load_sems,
    halo_send,
    halo_recv,
    edge_send,
    edge_recv,
    relay_send,
    relay_recv,
    out_send,
    out_recv,
    own_sem,
):
    me = lax.axis_index("tm")
    count = frames.shape[0]
    channels = frames.shape[-1]
    owned = result.shape[2]
    per_row = COLS // owned
    later = me + 1
    far = 1 - (2 * me) // n
    sign = 1 - 2 * far
    later_far = 1 - (2 * later) // n
    later_sign = 1 - 2 * later_far
    border = n // 2 - 1
    helper = max(border - 6, 0)

    def row_at(pos):
        return far * (ROWS - 1) + sign * pos

    def at_later(pos):
        return later_far * (ROWS - 1) + later_sign * row_at(pos)

    def from_later(pos):
        return far * (ROWS - 1) + sign * (later_far * (ROWS - 1) + later_sign * pos)

    loads = []
    for pos in range(ROWS):
        loads.append(
            pltpu.make_async_copy(
                frames_ref.at[:, row_at(pos)], frames.at[:, pos], frame_sems.at[pos]
            )
        )
    groups_one = []
    groups_two = []
    for source, target, groups in ((conv_one, kernel_one, groups_one), (conv_two, kernel_two, groups_two)):
        for tap in range(3):
            taps = pl.ds(3 * tap, 3)
            sem = load_sems.at[tap + 3 * (groups is groups_two)]
            groups.append(pltpu.make_async_copy(source.at[taps], target.at[taps], sem))
    project_load = pltpu.make_async_copy(out_weight, project, load_sems.at[6])
    for load in loads:
        load.start()
    for tap in (2, 1, 0):
        groups_one[tap].start()

    barrier = pltpu.get_barrier_semaphore()

    @pl.loop(1, n)
    def _(step):
        pl.semaphore_signal(
            barrier, inc=1, device_id={"tm": lax.rem(me + step, n)}, device_id_type=MESH
        )

    @pl.when(me == 0)
    def _():
        @pl.loop(0, 2 * ROWS)
        def _(index):
            blank = jnp.zeros((COLS, channels), jnp.bfloat16)
            halo[index // ROWS, index % ROWS] = blank
            edges[index // ROWS, index % ROWS] = blank

    gains_one = 0.5 * gain_one[...]
    gains_two = 0.5 * gain_two[...]

    def own_acts(pos):
        for frame in range(count - 1, -1, -1):
            act = norm_act(frames[frame, pos], gains_one)
            store_shifted(acts_one, frame + 2, pos, act)

    def to(device, source, target, send, recv):
        return pltpu.make_async_remote_copy(
            src_ref=source,
            dst_ref=target,
            send_sem=send,
            recv_sem=recv,
            device_id={"tm": lax.rem(device, n)},
            device_id_type=MESH,
        )

    def halo_copy(at, pos):
        source = frames.at[count - 2 + at, from_later(pos)]
        return to(later, source, halo.at[at, pos], halo_send, halo_recv.at[at, pos])

    def halo_to_relay(index):
        at, pos = RELAYED[index]
        source = frames.at[count - 2 + at, from_later(pos)]
        return to(helper, source, relay.at[index], halo_send, relay_recv.at[index])

    def relay_halo(index):
        at, pos = RELAYED[index]
        return to(border + 1, relay.at[index], halo.at[at, pos], relay_send, halo_recv.at[at, pos])

    def edge_source(pos):
        return first.at[pl.ds(count - 2, 2), pos]

    def edge_copy(pos):
        target = at_later(pos)
        return to(later, edge_source(pos), edges.at[:, target], edge_send, edge_recv.at[target])

    def relay_slot(index):
        return relay.at[pl.ds(len(RELAYED) + 2 * index, 2)]

    def edge_to_relay(pos, index):
        recv = relay_recv.at[len(RELAYED) + index]
        return to(helper, edge_source(pos), relay_slot(index), edge_send, recv)

    def relay_edge(index):
        pos = RELAYED_EDGES[index]
        return to(border + 1, relay_slot(index), edges.at[:, pos], relay_send, edge_recv.at[pos])

    def forward(halos, edges):
        @pl.when(me == helper)
        def _():
            for index in halos:
                slot = relay.at[index]
                pltpu.make_async_copy(slot, slot, relay_recv.at[index]).wait()
                relay_halo(index).start()
            for index in edges:
                slot = relay_slot(index)
                pltpu.make_async_copy(slot, slot, relay_recv.at[len(RELAYED) + index]).wait()
                relay_edge(index).start()

    def send_edges(positions):
        @pl.when(me == border)
        def _():
            for pos in positions:
                target = ROWS - 1 - pos
                if target in RELAYED_EDGES:
                    edge_to_relay(pos, RELAYED_EDGES.index(target)).start()
                else:
                    edge_copy(pos).start()

        @pl.when((later < n) & (me != border))
        def _():
            for pos in positions:
                edge_copy(pos).start()

    def conv(acts, kernel, frame, extent, pos, taps=(2, 1, 0), total=None):
        for tap in taps:
            for step in (0, 1, -1):
                if pos + step < 0 or pos + step >= ROWS:
                    continue
                window = acts[pl.ds(frame + tap, extent), pos + step]
                part = jnp.dot(
                    window.reshape(extent * COLS, 3 * channels),
                    kernel[tap * 3 + 1 + step * sign],
                    preferred_element_type=jnp.float32,
                )
                total = part if total is None else total + part
        return total

    pending = []

    def flush():
        for finish in pending:
            finish()
        pending.clear()

    def block(kind, frame, extent, pos):
        finish, acts, kernel = kind
        total = conv(acts, kernel, frame, extent, pos)
        flush()
        pending.append(lambda: finish(total, frame, extent, pos))

    def finish_one(total, frame, extent, pos):
        for at in range(extent):
            part = total[at * COLS : (at + 1) * COLS]
            value = (frames[frame + at, pos].astype(jnp.float32) + part).astype(jnp.bfloat16)
            first[frame + at, pos] = value
            store_shifted(acts_two, frame + at + 2, pos, norm_act(value, gains_two))

    def finish_two(total, frame, extent, pos):
        values = first[pl.ds(frame, extent), pos].reshape(extent * COLS, channels)
        value = (values.astype(jnp.float32) + total).astype(jnp.bfloat16)
        latent = jnp.dot(value, project[...], preferred_element_type=jnp.float32).astype(jnp.bfloat16)
        for at in range(extent):
            for index in range(per_row):
                begin = at * COLS + index * owned
                result[pos * per_row + index, frame + at] = latent[begin : begin + owned]
        own = ROWS // 2 <= pos
        for step in range(own, per_row):
            send(pos, lax.rem(me + step, per_row), frame, extent)

    one = (finish_one, acts_one, kernel_one)
    two = (finish_two, acts_two, kernel_two)

    def send(pos, index, frame, extent):
        to(
            row_at(pos) * per_row + index,
            result.at[pos * per_row + index, pl.ds(frame, extent)],
            out_ref.at[pl.ds(me * count + frame, extent)],
            out_send,
            out_recv,
        ).start()

    def wait_halo(at, positions):
        @pl.when(me > 0)
        def _():
            for pos in positions:
                slot = halo.at[at, pos]
                pltpu.make_async_copy(slot, slot, halo_recv.at[at, pos]).wait()

    def halo_acts(at, positions):
        for pos in positions:
            store_shifted(acts_one, at, pos, norm_act(halo[at, pos], gains_one))

    def wait_edges(positions):
        @pl.when(me > 0)
        def _():
            for pos in positions:
                slot = edges.at[:, pos]
                pltpu.make_async_copy(slot, slot, edge_recv.at[pos]).wait()

    def edge_acts(pos):
        for at in range(2):
            store_shifted(acts_two, at, pos, norm_act(edges[at, pos], gains_two))

    for load in loads:
        load.wait()
    own_acts(0)
    own_acts(1)
    pl.semaphore_wait(barrier, n - 1)

    @pl.when(me == border)
    def _():
        for index in range(len(RELAYED)):
            halo_to_relay(index).start()
        for at, pos in DIRECT:
            if (at, pos) not in RELAYED:
                halo_copy(at, pos).start()

    @pl.when((later < n) & (me != border))
    def _():
        for at, pos in DIRECT:
            halo_copy(at, pos).start()

    for group in groups_one:
        group.wait()
    for group in groups_two:
        group.start()
    project_load.start()

    last = count - 2
    block(one, last, 2, 0)
    own_acts(2)
    block(one, last, 2, 1)
    own_acts(3)
    block(one, last, 2, 2)
    block(one, last, 2, 3)
    flush()
    send_edges(range(ROWS))
    for frame in range(count - 3, -1, -1):
        if frame < 2:
            wait_halo(frame, (0, 1, 2))
            halo_acts(frame, (0, 1, 2))
        block(one, frame, 1, 0)
        block(one, frame, 1, 1)
        if frame == count - 3:
            for group in groups_two:
                group.wait()
            project_load.wait()
        flush()
        block(two, frame + 2, 1, 0)
        flush()
        if frame == count - 3:
            forward(range(len(RELAYED)), ())
    wait_halo(1, (3,))
    wait_halo(0, (3,))
    halo_acts(1, (3,))
    halo_acts(0, (3,))
    for frame in range(count - 4, -1, -2):
        block(one, frame, 2, 2)
    for frame in range(count - 4, -1, -2):
        block(one, frame, 2, 3)
    for frame in range(count - 2, 0, -2):
        block(two, frame, 2, 1)
    flush()
    forward((), range(len(RELAYED_EDGES)))
    wait_edges((0, 1))
    edge_acts(0)
    edge_acts(1)
    block(two, 0, 2, 0)
    for frame in range(count - 2, 0, -2):
        block(two, frame, 2, 2)
    flush()
    wait_edges((2, 3))
    edge_acts(2)
    block(two, 0, 2, 1)
    edge_acts(3)
    for frame in range(count - 2, 0, -2):
        block(two, frame, 2, 3)
    block(two, 0, 2, 2)
    block(two, 0, 2, 3)
    flush()

    for pos in range(ROWS // 2, ROWS):
        index = lax.rem(me, per_row)

        @pl.when(row_at(pos) * per_row + index != me)
        def _():
            send(pos, index, 0, count)

    mine = row_at(lax.rem(me // per_row, ROWS)) * per_row + lax.rem(me, per_row)
    own = pltpu.make_async_copy(
        result.at[mine], out_ref.at[pl.ds(me * count, count)], own_sem
    )
    own.start()

    @pl.when(later < n)
    def _():
        pltpu.make_async_copy(halo, halo, halo_send).wait()
        pltpu.make_async_copy(halo, halo, edge_send).wait()

    @pl.when(me == helper)
    def _():
        pltpu.make_async_copy(relay, relay, relay_send).wait()

    others = out_ref.at[pl.ds(0, (n - 1) * count)]
    sent = result.at[pl.ds(0, n - 1)]
    pltpu.make_async_copy(sent, sent, out_send).wait()
    pltpu.make_async_copy(others, others, out_recv).wait()
    own.wait()


def body(n, frames, gain_one, conv_one, gain_two, conv_two, out_weight):
    count, cells, channels = frames.shape
    owned = cells // n
    grid = (count, ROWS, COLS, channels)
    taps = (9, 3 * channels, channels)
    half = jnp.bfloat16
    hbm = pl.BlockSpec(memory_space=pl.ANY)
    vmem = pl.BlockSpec(memory_space=pltpu.VMEM)
    return pl.pallas_call(
        functools.partial(fused, n),
        out_shape=pltpu.VMEM((n * count, owned, channels), half),
        in_specs=[hbm, vmem, hbm, vmem, hbm, hbm],
        out_specs=hbm,
        scratch_shapes=[
            pltpu.VMEM(grid, half),
            pltpu.VMEM((2, ROWS, COLS, channels), half),
            pltpu.VMEM((2, ROWS, COLS, channels), half),
            pltpu.VMEM((len(RELAYED) + 2 * len(RELAYED_EDGES), COLS, channels), half),
            pltpu.VMEM(taps, half),
            pltpu.VMEM(taps, half),
            pltpu.VMEM((channels, channels), half),
            pltpu.VMEM((count + 2, ROWS, COLS, 3 * channels), half),
            pltpu.VMEM((count + 2, ROWS, COLS, 3 * channels), half),
            pltpu.VMEM(grid, half),
            pltpu.VMEM((n, count, owned, channels), half),
            pltpu.SemaphoreType.DMA((ROWS,)),
            pltpu.SemaphoreType.DMA((7,)),
            pltpu.SemaphoreType.DMA,
            pltpu.SemaphoreType.DMA((2, ROWS)),
            pltpu.SemaphoreType.DMA,
            pltpu.SemaphoreType.DMA((ROWS,)),
            pltpu.SemaphoreType.DMA,
            pltpu.SemaphoreType.DMA((len(RELAYED) + len(RELAYED_EDGES),)),
            pltpu.SemaphoreType.DMA,
            pltpu.SemaphoreType.DMA,
            pltpu.SemaphoreType.DMA,
        ],
        compiler_params=pltpu.CompilerParams(collective_id=0, has_side_effects=True),
    )(
        frames.reshape(grid),
        gain_one.reshape(1, channels),
        conv_one.reshape(taps),
        gain_two.reshape(1, channels),
        conv_two.reshape(taps),
        out_weight,
    )


def solution(mesh):
    placed = (P("tm", "clip", None), P(), P(), P(), P(), P())
    return jax.shard_map(
        functools.partial(body, mesh.shape["tm"]),
        mesh=mesh,
        in_specs=placed,
        out_specs=P(None, ("clip", "tm"), None),
        check_vma=False,
    )
```

time: 40.9 us -> 39.7 us (0.971)
  Pallas kernels: 39.5 us -> 38.2 us
    pallas_call x1, Pallas kernels: 39.5 us -> 38.2 us  [body(): pl.pallas_call(functools.partial(fused, n), out_shape=pltpu.VMEM((n * cou...]
where the time goes in v2:
time: 39.7 us; the launch traced here: 39.1 us
  Pallas kernels  38.2 us (96%)
  local copies, waits for them, and re-layouts  0.97 us (2%)
    pallas_call x1, Pallas kernels, body(): pl.pallas_call(functools.partial(fused, n), out_shape=pltpu.VMEM((n * cou...  38.2 us
    unnamed x1, local copies, waits for them, and re-layouts  0.97 us

profile of v2, /device:TPU:17, one launch (start us, length us, event | category | flops | bytes accessed | tf_op | source)
XLA Modules:
  0.0 39.1 jit_solution(10306491623154434482)
XLA Ops:
  0.0 38.2 %shard_map.64 = bf16[64,32,256]{2,1,0:T(8,128)(2,1)S(1)} custom-call(bf16[4,4,128,256]{3,2,1,0:T(8,128)(2,1)} %bitcast.7, f32[1,256]{1,0:T(1,128)} %bitcast.8, bf16[9,768,256]{2,1,0:T(8,128)(2,1)} %bitcast.5, f32[1,256]{1,0:T(1,128)} %bitcast.9, bf16[9,768,256]{2,1,0:T(8,128)(2,1)} %bitcast.6, bf16[256,256]{1,0:T(8,128)(2,1)} %out_weight.1), custom_call_target="tpu_custom_call" | custom-call | tf_op jit(solution)/shard_map/pallas_call | solution.py:396
  38.2 1.0 %copy.8 = bf16[64,32,256]{2,1,0:T(8,128)(2,1)} copy(bf16[64,32,256]{2,1,0:T(8,128)(2,1)S(1)} %shard_map.64) | data formatting | bytes 2097152

commit v3 on v2

--- a/solution.py
+++ b/solution.py
@@ -12,7 +12,7 @@
 MESH = pl.DeviceIdType.MESH
 DIRECT = ((1, 0), (1, 1), (1, 2), (0, 0), (0, 1), (0, 2), (1, 3), (0, 3))
 RELAYED = ((1, 3), (0, 3))
-RELAYED_EDGES = (3, 2)
+RELAYED_EDGES = (3,)
 
 
 def norm_act(x, half_gain):
@@ -75,7 +75,8 @@
     later_far = 1 - (2 * later) // n
     later_sign = 1 - 2 * later_far
     border = n // 2 - 1
-    helper = max(border - 6, 0)
+    routes = ((border, max(border - 6, 0)), (n // 4 - 1, max(n // 4 - 3, 0)))
+    crossing = (me == routes[0][0]) | (me == routes[1][0])
 
     def row_at(pos):
         return far * (ROWS - 1) + sign * pos
@@ -144,14 +145,17 @@
         source = frames.at[count - 2 + at, from_later(pos)]
         return to(later, source, halo.at[at, pos], halo_send, halo_recv.at[at, pos])
 
-    def halo_to_relay(index):
+    def halo_to_relay(route, index):
         at, pos = RELAYED[index]
         source = frames.at[count - 2 + at, from_later(pos)]
-        return to(helper, source, relay.at[index], halo_send, relay_recv.at[index])
-
-    def relay_halo(index):
+        recv = relay_recv.at[route, index]
+        return to(routes[route][1], source, relay.at[route, index], halo_send, recv)
+
+    def relay_halo(route, index):
         at, pos = RELAYED[index]
-        return to(border + 1, relay.at[index], halo.at[at, pos], relay_send, halo_recv.at[at, pos])
+        target = routes[route][0] + 1
+        recv = halo_recv.at[at, pos]
+        return to(target, relay.at[route, index], halo.at[at, pos], relay_send.at[route], recv)
 
     def edge_source(pos):
         return first.at[pl.ds(count - 2, 2), pos]
@@ -160,40 +164,47 @@
         target = at_later(pos)
         return to(later, edge_source(pos), edges.at[:, target], edge_send, edge_recv.at[target])
 
-    def relay_slot(index):
-        return relay.at[pl.ds(len(RELAYED) + 2 * index, 2)]
-
-    def edge_to_relay(pos, index):
-        recv = relay_recv.at[len(RELAYED) + index]
-        return to(helper, edge_source(pos), relay_slot(index), edge_send, recv)
-
-    def relay_edge(index):
+    def relay_slot(route, index):
+        return relay.at[route, pl.ds(len(RELAYED) + 2 * index, 2)]
+
+    def edge_to_relay(route, pos, index):
+        recv = relay_recv.at[route, len(RELAYED) + index]
+        return to(routes[route][1], edge_source(pos), relay_slot(route, index), edge_send, recv)
+
+    def relay_edge(route, index):
         pos = RELAYED_EDGES[index]
-        return to(border + 1, relay_slot(index), edges.at[:, pos], relay_send, edge_recv.at[pos])
-
-    def forward(halos, edges):
-        @pl.when(me == helper)
-        def _():
-            for index in halos:
-                slot = relay.at[index]
-                pltpu.make_async_copy(slot, slot, relay_recv.at[index]).wait()
-                relay_halo(index).start()
-            for index in edges:
-                slot = relay_slot(index)
-                pltpu.make_async_copy(slot, slot, relay_recv.at[len(RELAYED) + index]).wait()
-                relay_edge(index).start()
-
-    def send_edges(positions):
-        @pl.when(me == border)
-        def _():
-            for pos in positions:
-                target = ROWS - 1 - pos
-                if target in RELAYED_EDGES:
-                    edge_to_relay(pos, RELAYED_EDGES.index(target)).start()
-                else:
-                    edge_copy(pos).start()
-
-        @pl.when((later < n) & (me != border))
+        target = routes[route][0] + 1
+        recv = edge_recv.at[pos]
+        return to(target, relay_slot(route, index), edges.at[:, pos], relay_send.at[route], recv)
+
+    def forward(halos, edges_at):
+        for route in range(len(routes)):
+
+            @pl.when(me == routes[route][1])
+            def _():
+                for index in halos:
+                    slot = relay.at[route, index]
+                    pltpu.make_async_copy(slot, slot, relay_recv.at[route, index]).wait()
+                    relay_halo(route, index).start()
+                for index in edges_at:
+                    slot = relay_slot(route, index)
+                    recv = relay_recv.at[route, len(RELAYED) + index]
+                    pltpu.make_async_copy(slot, slot, recv).wait()
+                    relay_edge(route, index).start()
+
+    def send_edges(positions, here=True):
+        for route in range(len(routes)):
+
+            @pl.when((me == routes[route][0]) & here)
+            def _():
+                for pos in positions:
+                    target = pos if route else ROWS - 1 - pos
+                    if target in RELAYED_EDGES:
+                        edge_to_relay(route, pos, RELAYED_EDGES.index(target)).start()
+                    else:
+                        edge_copy(pos).start()
+
+        @pl.when((later < n) & jnp.logical_not(crossing) & here)
         def _():
             for pos in positions:
                 edge_copy(pos).start()
@@ -282,20 +293,27 @@
         load.wait()
     own_acts(0)
     own_acts(1)
-    pl.semaphore_wait(barrier, n - 1)
-
-    @pl.when(me == border)
-    def _():
-        for index in range(len(RELAYED)):
-            halo_to_relay(index).start()
-        for at, pos in DIRECT:
-            if (at, pos) not in RELAYED:
+    def enter(here):
+        @pl.when(here)
+        def _():
+            pl.semaphore_wait(barrier, n - 1)
+
+        for route in range(len(routes)):
+
+            @pl.when((me == routes[route][0]) & here)
+            def _():
+                for index in range(len(RELAYED)):
+                    halo_to_relay(route, index).start()
+                for at, pos in DIRECT:
+                    if (at, pos) not in RELAYED:
+                        halo_copy(at, pos).start()
+
+        @pl.when((later < n) & jnp.logical_not(crossing) & here)
+        def _():
+            for at, pos in DIRECT:
                 halo_copy(at, pos).start()
 
-    @pl.when((later < n) & (me != border))
-    def _():
-        for at, pos in DIRECT:
-            halo_copy(at, pos).start()
+    enter(me >= n // 4)
 
     for group in groups_one:
         group.wait()
@@ -304,14 +322,24 @@
     project_load.start()
 
     last = count - 2
+
+    def near_blocks(here):
+        @pl.when(here)
+        def _():
+            block(one, last, 2, 2)
+            block(one, last, 2, 3)
+            flush()
+
+        send_edges((2, 3), here)
+
     block(one, last, 2, 0)
     own_acts(2)
     block(one, last, 2, 1)
     own_acts(3)
-    block(one, last, 2, 2)
-    block(one, last, 2, 3)
     flush()
-    send_edges(range(ROWS))
+    enter(me < n // 4)
+    send_edges((0, 1))
+    near_blocks(me == border)
     for frame in range(count - 3, -1, -1):
         if frame < 2:
             wait_halo(frame, (0, 1, 2))
@@ -327,6 +355,7 @@
         flush()
         if frame == count - 3:
             forward(range(len(RELAYED)), ())
+    near_blocks(me != border)
     wait_halo(1, (3,))
     wait_halo(0, (3,))
     halo_acts(1, (3,))
@@ -335,23 +364,23 @@
         block(one, frame, 2, 2)
     for frame in range(count - 4, -1, -2):
         block(one, frame, 2, 3)
+    flush()
+    forward((), range(len(RELAYED_EDGES)))
     for frame in range(count - 2, 0, -2):
         block(two, frame, 2, 1)
     flush()
-    forward((), range(len(RELAYED_EDGES)))
     wait_edges((0, 1))
     edge_acts(0)
     edge_acts(1)
     block(two, 0, 2, 0)
-    for frame in range(count - 2, 0, -2):
-        block(two, frame, 2, 2)
+    for pos in (2, 3):
+        for frame in range(count - 2, 0, -2):
+            block(two, frame, 2, pos)
     flush()
     wait_edges((2, 3))
     edge_acts(2)
     block(two, 0, 2, 1)
     edge_acts(3)
-    for frame in range(count - 2, 0, -2):
-        block(two, frame, 2, 3)
     block(two, 0, 2, 2)
     block(two, 0, 2, 3)
     flush()
@@ -374,9 +403,11 @@
         pltpu.make_async_copy(halo, halo, halo_send).wait()
         pltpu.make_async_copy(halo, halo, edge_send).wait()
 
-    @pl.when(me == helper)
-    def _():
-        pltpu.make_async_copy(relay, relay, relay_send).wait()
+    for route in range(len(routes)):
+
+        @pl.when(me == routes[route][1])
+        def _():
+            pltpu.make_async_copy(relay.at[route], relay.at[route], relay_send.at[route]).wait()
 
     others = out_ref.at[pl.ds(0, (n - 1) * count)]
     sent = result.at[pl.ds(0, n - 1)]
@@ -402,7 +433,7 @@
             pltpu.VMEM(grid, half),
             pltpu.VMEM((2, ROWS, COLS, channels), half),
             pltpu.VMEM((2, ROWS, COLS, channels), half),
-            pltpu.VMEM((len(RELAYED) + 2 * len(RELAYED_EDGES), COLS, channels), half),
+            pltpu.VMEM((2, len(RELAYED) + 2 * len(RELAYED_EDGES), COLS, channels), half),
             pltpu.VMEM(taps, half),
             pltpu.VMEM(taps, half),
             pltpu.VMEM((channels, channels), half),
@@ -416,8 +447,8 @@
             pltpu.SemaphoreType.DMA((2, ROWS)),
             pltpu.SemaphoreType.DMA,
             pltpu.SemaphoreType.DMA((ROWS,)),
-            pltpu.SemaphoreType.DMA,
-            pltpu.SemaphoreType.DMA((len(RELAYED) + len(RELAYED_EDGES),)),
+            pltpu.SemaphoreType.DMA((2,)),
+            pltpu.SemaphoreType.DMA((2, len(RELAYED) + len(RELAYED_EDGES))),
             pltpu.SemaphoreType.DMA,
             pltpu.SemaphoreType.DMA,
             pltpu.SemaphoreType.DMA,

time: 39.7 us -> 37.7 us (0.950); the launches traced: 39.1 us -> 37.5 us
  Pallas kernels: 38.2 us -> 36.6 us
    pallas_call x1, Pallas kernels: 38.2 us -> 36.6 us  [body(): pl.pallas_call(functools.partial(fused, n), out_shape=pltpu.VMEM((n * cou...]
where the time goes in v3:
time: 37.7 us; the launch traced here: 37.5 us
  Pallas kernels  36.6 us (97%)
  local copies, waits for them, and re-layouts  0.97 us (3%)
    pallas_call x1, Pallas kernels, body(): pl.pallas_call(functools.partial(fused, n), out_shape=pltpu.VMEM((n * cou...  36.6 us
    unnamed x1, local copies, waits for them, and re-layouts  0.97 us

profile of v3, /device:TPU:17, one launch (start us, length us, event | category | flops | bytes accessed | tf_op | source)
XLA Modules:
  0.0 37.5 jit_solution(5206221396194984809)
XLA Ops:
  0.0 36.6 %shard_map.64 = bf16[64,32,256]{2,1,0:T(8,128)(2,1)S(1)} custom-call(bf16[4,4,128,256]{3,2,1,0:T(8,128)(2,1)} %bitcast.7, f32[1,256]{1,0:T(1,128)} %bitcast.8, bf16[9,768,256]{2,1,0:T(8,128)(2,1)} %bitcast.5, f32[1,256]{1,0:T(1,128)} %bitcast.9, bf16[9,768,256]{2,1,0:T(8,128)(2,1)} %bitcast.6, bf16[256,256]{1,0:T(8,128)(2,1)} %out_weight.1), custom_call_target="tpu_custom_call" | custom-call | tf_op jit(solution)/shard_map/pallas_call | solution.py:427
  36.6 1.0 %copy.8 = bf16[64,32,256]{2,1,0:T(8,128)(2,1)} copy(bf16[64,32,256]{2,1,0:T(8,128)(2,1)S(1)} %shard_map.64) | data formatting | bytes 2097152

commit v4 on v3

--- a/solution.py
+++ b/solution.py
@@ -209,8 +209,11 @@
             for pos in positions:
                 edge_copy(pos).start()
 
-    def conv(acts, kernel, frame, extent, pos, taps=(2, 1, 0), total=None):
-        for tap in taps:
+    def conv(acts, kernel, frame, extent, pos, arriving=None):
+        total = None
+        for tap in (2, 1, 0):
+            if arriving:
+                arriving[tap].wait()
             for step in (0, 1, -1):
                 if pos + step < 0 or pos + step >= ROWS:
                     continue
@@ -230,9 +233,9 @@
             finish()
         pending.clear()
 
-    def block(kind, frame, extent, pos):
+    def block(kind, frame, extent, pos, arriving=None):
         finish, acts, kernel = kind
-        total = conv(acts, kernel, frame, extent, pos)
+        total = conv(acts, kernel, frame, extent, pos, arriving)
         flush()
         pending.append(lambda: finish(total, frame, extent, pos))
 
@@ -315,31 +318,28 @@
 
     enter(me >= n // 4)
 
-    for group in groups_one:
-        group.wait()
+    last = count - 2
+
+    def near_blocks(here, positions):
+        @pl.when(here)
+        def _():
+            for pos in positions:
+                block(one, last, 2, pos)
+            flush()
+
+        send_edges(positions, here)
+
+    block(one, last, 2, 0, groups_one)
     for group in groups_two:
         group.start()
     project_load.start()
-
-    last = count - 2
-
-    def near_blocks(here):
-        @pl.when(here)
-        def _():
-            block(one, last, 2, 2)
-            block(one, last, 2, 3)
-            flush()
-
-        send_edges((2, 3), here)
-
-    block(one, last, 2, 0)
     own_acts(2)
     block(one, last, 2, 1)
     own_acts(3)
     flush()
     enter(me < n // 4)
     send_edges((0, 1))
-    near_blocks(me == border)
+    near_blocks(me == border, (2, 3))
     for frame in range(count - 3, -1, -1):
         if frame < 2:
             wait_halo(frame, (0, 1, 2))
@@ -355,20 +355,22 @@
         flush()
         if frame == count - 3:
             forward(range(len(RELAYED)), ())
-    near_blocks(me != border)
+    near_blocks(me != border, (2,))
     wait_halo(1, (3,))
     wait_halo(0, (3,))
     halo_acts(1, (3,))
     halo_acts(0, (3,))
     for frame in range(count - 4, -1, -2):
         block(one, frame, 2, 2)
+    flush()
+    for frame in range(count - 2, 0, -2):
+        block(two, frame, 2, 1)
+    flush()
+    near_blocks(me != border, (3,))
     for frame in range(count - 4, -1, -2):
         block(one, frame, 2, 3)
     flush()
     forward((), range(len(RELAYED_EDGES)))
-    for frame in range(count - 2, 0, -2):
-        block(two, frame, 2, 1)
-    flush()
     wait_edges((0, 1))
     edge_acts(0)
     edge_acts(1)

time: 37.7 us -> 37.7 us (level)
  no operation moved by 1% of the time
where the time goes in v4:
time: 37.7 us; the launch traced here: 37.6 us
  Pallas kernels  36.6 us (97%)
  local copies, waits for them, and re-layouts  0.97 us (3%)
    pallas_call x1, Pallas kernels, body(): pl.pallas_call(functools.partial(fused, n), out_shape=pltpu.VMEM((n * cou...  36.6 us
    unnamed x1, local copies, waits for them, and re-layouts  0.97 us

profile of v4, /device:TPU:17, one launch (start us, length us, event | category | flops | bytes accessed | tf_op | source)
XLA Modules:
  0.0 37.6 jit_solution(10881301049473856797)
XLA Ops:
  0.0 36.6 %shard_map.64 = bf16[64,32,256]{2,1,0:T(8,128)(2,1)S(1)} custom-call(bf16[4,4,128,256]{3,2,1,0:T(8,128)(2,1)} %bitcast.7, f32[1,256]{1,0:T(1,128)} %bitcast.8, bf16[9,768,256]{2,1,0:T(8,128)(2,1)} %bitcast.5, f32[1,256]{1,0:T(1,128)} %bitcast.9, bf16[9,768,256]{2,1,0:T(8,128)(2,1)} %bitcast.6, bf16[256,256]{1,0:T(8,128)(2,1)} %out_weight.1), custom_call_target="tpu_custom_call" | custom-call | tf_op jit(solution)/shard_map/pallas_call | solution.py:429
  36.6 1.0 %copy.8 = bf16[64,32,256]{2,1,0:T(8,128)(2,1)} copy(bf16[64,32,256]{2,1,0:T(8,128)(2,1)S(1)} %shard_map.64) | data formatting | bytes 2097152
